TPU v7x, 32 devices: a whole 2x2x4 slice. The times are simulated.
32 devices in a mesh: ga: 8 (over z, x), band: 4 (over y, core).
Axes of the slice: x: 2, y: 2, z: 4, core: 2. Of those that a mesh axis runs over, the one named last changes fastest.
Arguments:
- coeffs: bfloat16 [2, 512, 40960], P(None, ('ga', 'band')), may hold values from -6 to 6
- projectors: bfloat16 [1280, 2, 40960], P(None, None, 'ga'), may hold values from -0.01953125 to 0.01953125
- block_coupling: float32 [1280, 18], replicated, may hold values from -12 to 12
- atom_counts: int32 [160], replicated, may hold values from 4 to 18, as said below
- wave_counts: int32 [8], P('ga'), may hold values from 3840 to 5120
Outputs:
- applied: bfloat16 [2, 512, 40960], P(None, ('ga', 'band'))
- band_energy: float32 [512], P(('ga', 'band'))
- total_energy: float32 [], replicated
Inputs may be any that keep to these rules, and one draw needn't show every extreme that they name: `atom_counts`: each atom has 4, 8 or 18 projectors, the counts sum to 1280 and the largest is 18.
All inputs are finite; a program needn't handle non-finite values.
Results may differ from a plain program's by a relative error of at most 0.013.
Values may be sent and summed in bfloat16 or wider, within the bound.
A program may use at most 128 MiB of HBM per device.

v0:
```python
import math
import jax
import jax.numpy as jnp
from jax import lax
from jax.sharding import PartitionSpec as P


def block_tables(atom_counts, row_ids):
    atom_ends = jnp.cumsum(atom_counts)
    atom_starts = atom_ends - atom_counts
    inside = (atom_starts[None, :] <= row_ids[:, None]) & (atom_ends[None, :] > row_ids[:, None])
    block_first = jnp.sum(jnp.where(inside, atom_starts[None, :], 0), axis=1)
    block_length = jnp.sum(jnp.where(inside, atom_counts[None, :], 0), axis=1)
    return (block_first, block_length)


def coupling_matrix(block_first, block_length, coupling_rows, column_count):
    column_ids = lax.iota(jnp.int32, column_count)
    offsets = column_ids[None, :] - block_first[:, None]
    matrix = jnp.zeros((coupling_rows.shape[0], column_count), jnp.float32)
    for offset in range(coupling_rows.shape[1]):
        hit = (offsets == offset) & (offset < block_length[:, None])
        matrix = jnp.where(hit, coupling_rows[:, offset : offset + 1], matrix)
    return matrix


def shards(coeffs, projectors, block_coupling, atom_counts, wave_counts):
    moved_bands = lax.all_to_all(coeffs, "ga", split_axis=2, concat_axis=1, tiled=True)
    own_bands = coeffs.shape[1]
    group_bands = moved_bands.shape[1]
    wave_slots = projectors.shape[2]
    proj_total_rows = projectors.shape[0]
    in_sphere = (lax.iota(jnp.int32, wave_slots) < wave_counts[0]).astype(jnp.float32)
    masked = moved_bands * in_sphere.astype(jnp.bfloat16)
    real_part = masked[0]
    imag_part = masked[1]
    stacked = jnp.concatenate(
        [jnp.concatenate([real_part, imag_part], 1), jnp.concatenate([imag_part, -real_part], 1)], 0
    )
    flat_beta = projectors.reshape(proj_total_rows, 2 * wave_slots)
    contract_last = (((1,), (1,)), ((), ()))
    contract_first = (((0,), (0,)), ((), ()))
    ga_index = lax.axis_index("ga")
    local_terms = lax.dot_general(
        flat_beta, stacked, contract_last, preferred_element_type=jnp.float32
    )
    projections = lax.psum(local_terms, "ga")
    block_first, block_length = block_tables(atom_counts, lax.iota(jnp.int32, proj_total_rows))
    matrix = coupling_matrix(block_first, block_length, block_coupling, proj_total_rows)
    coupled = jnp.dot(
        matrix, projections, precision=lax.Precision.HIGHEST, preferred_element_type=jnp.float32
    )
    energy_terms = jnp.sum(projections * coupled, axis=0)
    group_energy = (energy_terms[:group_bands] + energy_terms[group_bands:]) / proj_total_rows
    band_energy = lax.dynamic_slice_in_dim(group_energy, ga_index * own_bands, own_bands, 0)
    total_energy = lax.psum(jnp.sum(group_energy), "band")
    products = lax.dot_general(
        coupled.astype(jnp.bfloat16), flat_beta, contract_first, preferred_element_type=jnp.float32
    )
    band_total = own_bands * lax.axis_size("ga") * lax.axis_size("band")
    total_energy = total_energy / math.sqrt(band_total)
    real_out = products[:group_bands, :wave_slots] - products[group_bands:, wave_slots:]
    imag_out = products[:group_bands, wave_slots:] + products[group_bands:, :wave_slots]
    result = (jnp.stack([real_out, imag_out]) * in_sphere).astype(jnp.bfloat16)
    applied = lax.all_to_all(result, "ga", split_axis=1, concat_axis=2, tiled=True)
    return (applied, band_energy, total_energy)


def solution(mesh):
    placed = (P(None, ("ga", "band"), None), P(None, None, "ga"), P(), P(), P("ga"))
    return jax.shard_map(
        shards,
        mesh=mesh,
        in_specs=placed,
        out_specs=(P(None, ("ga", "band"), None), P(("ga", "band")), P()),
        check_vma=False,
    )
```

profile of v0, /device:TPU:0, one launch (start us, length us, event | category | flops | bytes accessed | tf_op | source)
XLA Modules:
  0.0 439.4 jit_solution(13984395675737779399)
XLA Ops:
  7.2 38.0 %copy.21 = bf16[2,16,40960]{1,0,2:T(2,128)(2,1)} copy(bf16[2,16,40960]{2,1,0:T(8,128)(2,1)} %param.5) | data formatting | bytes 5242880 | tf_op args[0]
  45.1 24.1 %reshape.129 = bf16[8,2,81920]{2,1,0:T(2,128)(2,1)} reshape(bf16[40960,2,16]{2,1,0:T(2,128)(2,1)} %bitcast.40) | data formatting | bytes 5242880
  69.2 7.3 %all-to-all-start = ((bf16[8,2,81920]{2,1,0:T(2,128)(2,1)}), bf16[8,2,81920]{2,1,0:T(2,128)(2,1)S(1)}, u32[]{:S(2)}, u32[]{:S(2)}) async-start(bf16[8,2,81920]{2,1,0:T(2,128)(2,1)} %reshape.129), calls=%async_computation | async-start | bytes 5242880 | tf_op jit(solution)/shard_map/all_to_all | solution.py:28
  76.5 0.4 all-reduce.3.cloned.1.call-start
  77.6 23.8 %copy.29 = bf16[160,8,2,5120]{3,1,2,0:T(8,128)(2,1)} copy(bf16[160,8,2,5120]{3,2,1,0:T(2,128)(2,1)} %bitcast.41) | data formatting | bytes 52428800
  101.3 34.6 %all-to-all-done = bf16[8,2,81920]{2,1,0:T(2,128)(2,1)S(1)} async-done(((bf16[8,2,81920]{2,1,0:T(2,128)(2,1)}), bf16[8,2,81920]{2,1,0:T(2,128)(2,1)S(1)}, u32[]{:S(2)}, u32[]{:S(2)}) %all-to-all-start) | async-done | bytes 2621472 | tf_op jit(solution)/shard_map/all_to_all | solution.py:28
  136.0 17.1 %reshape.130 = bf16[40960,2,16]{2,1,0:T(2,128)(2,1)} reshape(bf16[8,2,81920]{2,1,0:T(2,128)(2,1)S(1)} %all-to-all-done) | data formatting | bytes 5242880
  153.0 37.5 %copy.28 = bf16[2,16,8,5120]{3,1,2,0:T(8,128)(2,1)S(1)} copy(bf16[2,16,8,5120]{1,0,3,2:T(2,128)(2,1)} %bitcast.39) | data formatting | bytes 5242880 | tf_op jit(solution)/shard_map/all_to_all | solution.py:28
  190.5 0.3 bitcast_multiply_fusion
  190.9 0.2 slice_bitcast_fusion.1
  191.1 0.1 fusion.168
  191.2 0.0 copy-start.1
  191.2 0.0 copy-start
  191.2 28.8 %fusion.138 = f32[1280,256]{0,1:T(8,128)} fusion(bf16[1280,10240]{1,0:T(8,128)(2,1)} %bitcast.37, bf16[128,5120]{1,0:T(8,128)(2,1)S(1)} %fusion.168, bf16[128,5120]{1,0:T(8,128)(2,1)S(1)} %get-tuple-element.28, bf16[128,5120]{1,0:T(8,128)(2,1)S(1)} %get-tuple-element.27), kind=kOutput, calls=%fused_computation.122 | convolution fusion | flops 6731857920 | bytes 31457280 | tf_op jit(solution)/shard_map/dot_general | solution.py:44
  220.0 0.0 all-reduce.3.cloned.1.call-update
  220.1 0.0 copy-done.1
  220.1 0.3 reduce-window.9
  220.4 0.1 slice.88
  220.5 0.1 slice_reduce_fusion.18
  220.6 0.0 copy-done
  220.6 0.2 slice_reduce_fusion.17
  220.9 0.1 add_bitcast_fusion
  220.9 0.3 select_reduce_fusion
  221.3 81.6 %all-reduce.3.cloned.1.call-done = f32[1280,256]{0,1:T(8,128)} async-done(((f32[1280,256]{0,1:T(8,128)}), f32[1280,256]{0,1:T(8,128)}) %all-reduce.3.cloned.1.call-update) | async-done | bytes 1310736 | tf_op jit(solution)/shard_map/psum | solution.py:47
  303.0 39.1 %fusion = f32[1280,256]{1,0:T(8,128)} fusion(f32[1280,256]{0,1:T(8,128)} %all-reduce.3.cloned.1.call-done, f32[1280]{0:T(1024)S(1)} %get-tuple-element.19, f32[1280]{0:T(1024)S(1)} %get-tuple-element.20, f32[1280]{0:T(1024)S(1)} %get-tuple-element.4, f32[1280]{0:T(1024)S(1)} %get-tuple-element.5, f32[1280]{0:T(1024)S(1)} %get-tuple-element.6, ...), kind=kOutput, calls=%fused_computation | convolution fusion | flops 5123276800 | bytes 2741760 | tf_op jit(solution)/shard_map/dot_general | solution.py:50
  342.1 13.0 %fusion.144 = f32[256,10240]{1,0:T(8,128)S(1)} fusion(bf16[1280,10240]{1,0:T(8,128)(2,1)} %bitcast.38, f32[1280,256]{1,0:T(8,128)} %fusion), kind=kOutput, calls=%fused_computation.136 | convolution fusion | flops 6711214080 | bytes 38010880 | tf_op jit(solution)/shard_map/dot_general | solution.py:57
  355.1 0.8 fusion.142
  355.9 0.5 fusion.81
  356.4 4.2 copy.24
  360.6 3.7 all-to-all-start.1
  364.2 2.8 copy.26
  367.0 1.9 multiply_reduce_fusion
  368.9 0.6 fusion.169
  369.5 7.3 %psum.15 = f32[]{:T(128)} all-reduce(f32[]{:T(128)} %get-tuple-element.23), channel_id=1, replica_groups=mesh['ga'=8,'band'=4] {'band'}, use_global_device_ids=true, to_apply=%region_7.8 | all-reduce | flops 1 | bytes 8 | tf_op jit(solution)/shard_map/psum | solution.py:56
  376.9 0.6 dynamic_slice.3
  378.1 45.7 %all-to-all-done.1 = bf16[2,128,5120]{2,0,1:T(2,128)(2,1)S(1)} async-done(((bf16[2,128,5120]{2,0,1:T(2,128)(2,1)}), bf16[2,128,5120]{2,0,1:T(2,128)(2,1)S(1)}, u32[]{:S(2)}, u32[]{:S(2)}) %all-to-all-start.1) | async-done | bytes 2621472 | tf_op jit(solution)/shard_map/all_to_all | solution.py:65
  423.8 2.9 copy.25
  426.7 4.5 %all_to_all.33 = bf16[2,16,40960]{2,1,0:T(8,128)(2,1)} reshape(bf16[2,16,8,5120]{3,2,1,0:T(8,128)(2,1)} %copy.25) | data formatting | bytes 5242880 | tf_op jit(solution)/shard_map/all_to_all | solution.py:65
  (5 shorter events, 0.1 us)
Async XLA Ops:
  69.2 66.8 %all-to-all-start = ((bf16[8,2,81920]{2,1,0:T(2,128)(2,1)}), bf16[8,2,81920]{2,1,0:T(2,128)(2,1)S(1)}, u32[]{:S(2)}, u32[]{:S(2)}) async-start(bf16[8,2,81920]{2,1,0:T(2,128)(2,1)} %reshape.129), calls=%async_computation | async-start | bytes 5242880 | tf_op jit(solution)/shard_map/all_to_all | solution.py:28
  76.5 226.5 %all-reduce.3.cloned.1.call-start = ((), (), s32[]{:S(2)}) async-start(), calls=%async_computation.2 | async-start | bytes 2621440 | tf_op jit(solution)/shard_map/psum | solution.py:47
  191.2 28.9 %copy-start.1 = (s32[160]{0:T(256)S(1)}, s32[160]{0:T(256)}, u32[]{:S(2)}) copy-start(s32[160]{0:T(256)} %param.8) | copy-start | bytes 1924
  191.2 29.4 %copy-start = (f32[1280,18]{0,1:T(8,128)S(1)}, f32[1280,18]{0,1:T(8,128)}, u32[]{:S(2)}) copy-start(f32[1280,18]{0,1:T(8,128)} %param.7) | copy-start | bytes 276484
  360.6 63.2 %all-to-all-start.1 = ((bf16[2,128,5120]{2,0,1:T(2,128)(2,1)}), bf16[2,128,5120]{2,0,1:T(2,128)(2,1)S(1)}, u32[]{:S(2)}, u32[]{:S(2)}) async-start(bf16[2,128,5120]{2,0,1:T(2,128)(2,1)} %copy.24), calls=%async_computation.1 | async-start | bytes 5242880 | tf_op jit(solution)/shard_map/all_to_all | solution.py:65
Sparse Core Ops, SparseCore 0:
  220.2 82.7 all-reduce.2
where the time goes:
time: 447 us; the launch traced here: 439 us
  waiting for transfers between devices  162 us (36%)
  local copies, waits for them, and re-layouts  156 us (35%)
  matrix products  81 us (18%)
  between operations  16.8 us (4%)
  starting transfers between devices  11.4 us (3%)
  blocking collectives  7.33 us (2%)
  other arithmetic  4.94 us (1%)
    unnamed x8, local copies, waits for them, and re-layouts  103 us
    psum x1, waiting for transfers between devices, shards(): projections = lax.psum(local_terms, 'ga')  81.6 us
    all_to_all x1, waiting for transfers between devices, shards(): lax.all_to_all(result, 'ga', split_axis=1, concat_axis=2, tiled=True)  45.7 us
    dot_general x1, matrix products, shards(): jnp.dot(matrix, projections, precision=lax.Precision.HIGHEST, preferred_e...  39.1 us
    all_to_all x1, local copies, waits for them, and re-layouts, shards(): lax.all_to_all(coeffs, 'ga', split_axis=2, concat_axis=1, tiled=True)  37.5 us
    all_to_all x1, waiting for transfers between devices, shards(): lax.all_to_all(coeffs, 'ga', split_axis=2, concat_axis=1, tiled=True)  34.6 us
    dot_general x1, matrix products, shards(): lax.dot_general(flat_beta, stacked, contract_last, preferred_element_type...  28.8 us
    dot_general x1, matrix products, shards(): lax.dot_general(coupled.astype(jnp.bfloat16), flat_beta, contract_first,...  13 us
  transfers between devices with their start and end apart: 3, of which 3 were waited for; matrix products, arithmetic and copies ran while one was open for 7% of the time, Pallas kernels for 0%

commit v1 on v0

--- a/solution.py
+++ b/solution.py
@@ -44,7 +44,11 @@
     local_terms = lax.dot_general(
         flat_beta, stacked, contract_last, preferred_element_type=jnp.float32
     )
-    projections = lax.psum(local_terms, "ga")
+    projections = local_terms
+    for hop in (1, 2, 4):
+        projections = projections + lax.ppermute(
+            projections, "ga", [(dev, dev ^ hop) for dev in range(8)]
+        )
     block_first, block_length = block_tables(atom_counts, lax.iota(jnp.int32, proj_total_rows))
     matrix = coupling_matrix(block_first, block_length, block_coupling, proj_total_rows)
     coupled = jnp.dot(

time: 447 us -> 469 us (1.049)
  waiting for transfers between devices: 162 us -> 191 us
  between operations: 16.8 us -> 3.43 us
  starting transfers between devices: 11.4 us -> 18.2 us
    ppermute x0 -> x3, waiting for transfers between devices: none -> 111 us  [shards(): lax.ppermute(projections, 'ga', [(dev, dev ^ hop) for dev in range(8)])]
    psum x1 -> x0, waiting for transfers between devices: 81.6 us -> none  [shards(): projections = lax.psum(local_terms, 'ga')]
    ppermute x0 -> x3, starting transfers between devices: none -> 5.68 us  [shards(): lax.ppermute(projections, 'ga', [(dev, dev ^ hop) for dev in range(8)])]
    unnamed x8 -> x10, local copies, waits for them, and re-layouts: 103 us -> 104 us
  transfers between devices with their start and end apart: 3 -> 5, of which waited for: 3 -> 5; matrix products, arithmetic and copies ran while one was open for 7% -> 7% of each run, Pallas kernels for 0% -> 0%
where the time goes in v1:
time: 469 us; the launch traced here: 461 us
  waiting for transfers between devices  191 us (41%)
  local copies, waits for them, and re-layouts  157 us (33%)
  matrix products  78.7 us (17%)
  starting transfers between devices  18.2 us (4%)
  blocking collectives  7.41 us (2%)
  other arithmetic  5.39 us (1%)
    ppermute x3, waiting for transfers between devices, shards(): lax.ppermute(projections, 'ga', [(dev, dev ^ hop) for dev in range(8)])  111 us
    unnamed x10, local copies, waits for them, and re-layouts  104 us
    all_to_all x1, waiting for transfers between devices, shards(): lax.all_to_all(result, 'ga', split_axis=1, concat_axis=2, tiled=True)  45.7 us
    dot_general x1, matrix products, shards(): jnp.dot(matrix, projections, precision=lax.Precision.HIGHEST, preferred_e...  37.9 us
    all_to_all x1, local copies, waits for them, and re-layouts, shards(): lax.all_to_all(coeffs, 'ga', split_axis=2, concat_axis=1, tiled=True)  37.5 us
    all_to_all x1, waiting for transfers between devices, shards(): lax.all_to_all(coeffs, 'ga', split_axis=2, concat_axis=1, tiled=True)  35 us
    dot_general x1, matrix products, shards(): lax.dot_general(flat_beta, stacked, contract_last, preferred_element_type...  27.8 us
    dot_general x1, matrix products, shards(): lax.dot_general(coupled.astype(jnp.bfloat16), flat_beta, contract_first,...  13 us
  transfers between devices with their start and end apart: 5, of which 5 were waited for; matrix products, arithmetic and copies ran while one was open for 7% of the time, Pallas kernels for 0%

profile of v1, /device:TPU:0, one launch (start us, length us, event | category | flops | bytes accessed | tf_op | source)
XLA Modules:
  0.0 461.4 jit_solution(2564692843952915864)
XLA Ops:
  0.6 38.0 %copy.21 = bf16[2,16,40960]{1,0,2:T(2,128)(2,1)} copy(bf16[2,16,40960]{2,1,0:T(8,128)(2,1)} %param.5) | data formatting | bytes 5242880 | tf_op args[0]
  38.6 24.1 %reshape.129 = bf16[8,2,81920]{2,1,0:T(2,128)(2,1)} reshape(bf16[40960,2,16]{2,1,0:T(2,128)(2,1)} %bitcast.40) | data formatting | bytes 5242880
  62.7 7.7 %all-to-all-start = ((bf16[8,2,81920]{2,1,0:T(2,128)(2,1)}), bf16[8,2,81920]{2,1,0:T(2,128)(2,1)S(1)}, u32[]{:S(2)}, u32[]{:S(2)}) async-start(bf16[8,2,81920]{2,1,0:T(2,128)(2,1)} %reshape.129), calls=%async_computation | async-start | bytes 5242880 | tf_op jit(solution)/shard_map/all_to_all | solution.py:28
  71.0 23.8 %copy.29 = bf16[160,8,2,5120]{3,1,2,0:T(8,128)(2,1)} copy(bf16[160,8,2,5120]{3,2,1,0:T(2,128)(2,1)} %bitcast.41) | data formatting | bytes 52428800
  94.8 35.0 %all-to-all-done = bf16[8,2,81920]{2,1,0:T(2,128)(2,1)S(1)} async-done(((bf16[8,2,81920]{2,1,0:T(2,128)(2,1)}), bf16[8,2,81920]{2,1,0:T(2,128)(2,1)S(1)}, u32[]{:S(2)}, u32[]{:S(2)}) %all-to-all-start) | async-done | bytes 2621472 | tf_op jit(solution)/shard_map/all_to_all | solution.py:28
  129.8 17.1 %reshape.130 = bf16[40960,2,16]{2,1,0:T(2,128)(2,1)} reshape(bf16[8,2,81920]{2,1,0:T(2,128)(2,1)S(1)} %all-to-all-done) | data formatting | bytes 5242880
  146.9 37.5 %copy.28 = bf16[2,16,8,5120]{3,1,2,0:T(8,128)(2,1)S(1)} copy(bf16[2,16,8,5120]{1,0,3,2:T(2,128)(2,1)} %bitcast.39) | data formatting | bytes 5242880 | tf_op jit(solution)/shard_map/all_to_all | solution.py:28
  184.4 0.3 bitcast_multiply_fusion
  184.7 0.2 slice_bitcast_fusion.1
  184.9 0.1 fusion.168
  185.0 27.8 %fusion.138 = f32[1280,256]{0,1:T(8,128)S(1)} fusion(bf16[1280,10240]{1,0:T(8,128)(2,1)} %bitcast.37, bf16[128,5120]{1,0:T(8,128)(2,1)S(1)} %fusion.168, bf16[128,5120]{1,0:T(8,128)(2,1)S(1)} %get-tuple-element.28, bf16[128,5120]{1,0:T(8,128)(2,1)S(1)} %get-tuple-element.27), kind=kOutput, calls=%fused_computation.122 | convolution fusion | flops 6731857920 | bytes 31457280 | tf_op jit(solution)/shard_map/dot_general | solution.py:44
  212.8 1.5 collective-permute-start
  214.3 28.1 %collective-permute-done = f32[1280,256]{0,1:T(8,128)S(1)} collective-permute-done((f32[1280,256]{0,1:T(8,128)S(1)}, f32[1280,256]{0,1:T(8,128)S(1)}, u32[]{:S(2)}, u32[]{:S(2)}) %collective-permute-start) | collective-permute-done | bytes 1310752 | tf_op jit(solution)/shard_map/ppermute | solution.py:49
  242.3 0.2 add.22
  242.5 0.0 copy-start.2
  242.5 0.0 copy-start.1
  242.6 0.8 collective-permute-start.1
  243.4 28.1 %collective-permute-done.1 = f32[1280,256]{0,1:T(8,128)S(1)} collective-permute-done((f32[1280,256]{0,1:T(8,128)S(1)}, f32[1280,256]{0,1:T(8,128)S(1)}, u32[]{:S(2)}, u32[]{:S(2)}) %collective-permute-start.1) | collective-permute-done | bytes 1310752 | tf_op jit(solution)/shard_map/ppermute | solution.py:49
  271.5 0.1 add.23
  271.6 3.3 collective-permute-start.2
  274.9 0.0 copy-done.2
  275.0 0.3 reduce-window.9
  275.3 0.1 slice.88
  275.4 0.1 slice_reduce_fusion.18
  275.5 0.0 copy-done.1
  275.5 0.3 slice_reduce_fusion.17
  275.7 0.1 add_bitcast_fusion
  275.8 0.3 select_reduce_fusion
  276.2 54.4 %collective-permute-done.2 = f32[1280,256]{0,1:T(8,128)S(1)} collective-permute-done((f32[1280,256]{0,1:T(8,128)S(1)}, f32[1280,256]{0,1:T(8,128)S(1)}, u32[]{:S(2)}, u32[]{:S(2)}) %collective-permute-start.2) | collective-permute-done | bytes 1310752 | tf_op jit(solution)/shard_map/ppermute | solution.py:49
  330.6 0.1 add.24
  330.7 0.0 copy-start
  330.7 1.0 copy-done
  331.8 37.9 %fusion = f32[1280,256]{1,0:T(8,128)} fusion(f32[1280,256]{0,1:T(8,128)S(1)} %add.24, f32[1280]{0:T(1024)S(1)} %get-tuple-element.19, f32[1280]{0:T(1024)S(1)} %get-tuple-element.20, f32[1280]{0:T(1024)S(1)} %get-tuple-element.4, f32[1280]{0:T(1024)S(1)} %get-tuple-element.5, f32[1280]{0:T(1024)S(1)} %get-tuple-element.6, f32[1280]{0:T(1024)S(1)} %get-tuple-element.7, ...), kind=kOutput, calls=%fused_computation | convolution fusion | flops 5123276800 | bytes 2741760 | tf_op jit(solution)/shard_map/dot_general | solution.py:54
  369.7 13.0 %fusion.144 = f32[256,10240]{1,0:T(8,128)S(1)} fusion(bf16[1280,10240]{1,0:T(8,128)(2,1)} %bitcast.38, f32[1280,256]{1,0:T(8,128)} %fusion), kind=kOutput, calls=%fused_computation.136 | convolution fusion | flops 6711214080 | bytes 38010880 | tf_op jit(solution)/shard_map/dot_general | solution.py:61
  382.7 0.8 fusion.142
  383.5 0.5 fusion.81
  383.9 4.2 copy.24
  388.1 4.9 %all-to-all-start.1 = ((bf16[2,128,5120]{2,0,1:T(2,128)(2,1)}), bf16[2,128,5120]{2,0,1:T(2,128)(2,1)S(1)}, u32[]{:S(2)}, u32[]{:S(2)}) async-start(bf16[2,128,5120]{2,0,1:T(2,128)(2,1)} %copy.24), calls=%async_computation.1 | async-start | bytes 5242880 | tf_op jit(solution)/shard_map/all_to_all | solution.py:69
  393.0 2.8 copy.26
  395.8 1.9 multiply_reduce_fusion
  397.7 0.6 fusion.169
  398.3 7.4 %psum.7 = f32[]{:T(128)} all-reduce(f32[]{:T(128)} %get-tuple-element.23), channel_id=1, replica_groups=mesh['ga'=8,'band'=4] {'band'}, use_global_device_ids=true, to_apply=%region_6.7 | all-reduce | flops 1 | bytes 8 | tf_op jit(solution)/shard_map/psum | solution.py:60
  405.7 0.6 dynamic_slice.3
  406.9 45.7 %all-to-all-done.1 = bf16[2,128,5120]{2,0,1:T(2,128)(2,1)S(1)} async-done(((bf16[2,128,5120]{2,0,1:T(2,128)(2,1)}), bf16[2,128,5120]{2,0,1:T(2,128)(2,1)S(1)}, u32[]{:S(2)}, u32[]{:S(2)}) %all-to-all-start.1) | async-done | bytes 2621472 | tf_op jit(solution)/shard_map/all_to_all | solution.py:69
  452.7 2.9 copy.25
  455.6 4.5 all_to_all.33
  (5 shorter events, 0.1 us)
Async XLA Ops:
  62.7 67.1 %all-to-all-start = ((bf16[8,2,81920]{2,1,0:T(2,128)(2,1)}), bf16[8,2,81920]{2,1,0:T(2,128)(2,1)S(1)}, u32[]{:S(2)}, u32[]{:S(2)}) async-start(bf16[8,2,81920]{2,1,0:T(2,128)(2,1)} %reshape.129), calls=%async_computation | async-start | bytes 5242880 | tf_op jit(solution)/shard_map/all_to_all | solution.py:28
  212.8 29.6 %collective-permute-start = (f32[1280,256]{0,1:T(8,128)S(1)}, f32[1280,256]{0,1:T(8,128)S(1)}, u32[]{:S(2)}, u32[]{:S(2)}) collective-permute-start(f32[1280,256]{0,1:T(8,128)S(1)} %fusion.138), channel_id=1, source_target_pairs={{0,4},{4,0},{8,12},{12,8},{16,20},{20,16},{24,28},{28,24},{1,5},{5... | collective-permute-start | bytes 3932168 | tf_op jit(solution)/shard_map/ppermute | solution.py:49
  242.5 32.4 %copy-start.2 = (s32[160]{0:T(256)S(1)}, s32[160]{0:T(256)}, u32[]{:S(2)}) copy-start(s32[160]{0:T(256)} %param.8) | copy-start | bytes 1924
  242.5 33.0 %copy-start.1 = (f32[1280,18]{0,1:T(8,128)S(1)}, f32[1280,18]{0,1:T(8,128)}, u32[]{:S(2)}) copy-start(f32[1280,18]{0,1:T(8,128)} %param.7) | copy-start | bytes 276484
  242.6 28.9 %collective-permute-start.1 = (f32[1280,256]{0,1:T(8,128)S(1)}, f32[1280,256]{0,1:T(8,128)S(1)}, u32[]{:S(2)}, u32[]{:S(2)}) collective-permute-start(f32[1280,256]{0,1:T(8,128)S(1)} %add.22), channel_id=1, source_target_pairs={{0,8},{4,12},{8,0},{12,4},{16,24},{20,28},{24,16},{28,20},{1,9},{5... | collective-permute-start | bytes 3932168 | tf_op jit(solution)/shard_map/ppermute | solution.py:49
  271.6 59.0 %collective-permute-start.2 = (f32[1280,256]{0,1:T(8,128)S(1)}, f32[1280,256]{0,1:T(8,128)S(1)}, u32[]{:S(2)}, u32[]{:S(2)}) collective-permute-start(f32[1280,256]{0,1:T(8,128)S(1)} %add.23), channel_id=1, source_target_pairs={{0,16},{4,20},{8,24},{12,28},{16,0},{20,4},{24,8},{28,12},{1,17},{... | collective-permute-start | bytes 3932168 | tf_op jit(solution)/shard_map/ppermute | solution.py:49
  330.7 1.1 copy-start
  388.1 64.5 %all-to-all-start.1 = ((bf16[2,128,5120]{2,0,1:T(2,128)(2,1)}), bf16[2,128,5120]{2,0,1:T(2,128)(2,1)S(1)}, u32[]{:S(2)}, u32[]{:S(2)}) async-start(bf16[2,128,5120]{2,0,1:T(2,128)(2,1)} %copy.24), calls=%async_computation.1 | async-start | bytes 5242880 | tf_op jit(solution)/shard_map/all_to_all | solution.py:69
